TPU v7x, 32 devices: a 4x2x2 block of a 4x4x8 slice. The times are simulated.
32 devices in a mesh: dp: 4 (over y, z), tp: 8 (over x, core).
Axes of the slice: x: 4, y: 2, z: 2, core: 2. Of those that a mesh axis runs over, the one named last changes fastest.
The devices are a block of a 4x4x8 slice.
Arguments:
- hidden: bfloat16 [4, 256, 5120], P('dp', 'tp'), parts along dimension 0
- ln1_gain: float32 [5120], replicated
- ln1_bias: float32 [5120], replicated
- w_qkv: bfloat16 [5120, 3, 40, 128], P(None, None, 'tp')
- b_qkv: bfloat16 [3, 40, 128], P(None, 'tp')
- w_out: bfloat16 [40, 128, 5120], P('tp')
- b_out: bfloat16 [5120], replicated
- ln2_gain: float32 [5120], replicated
- ln2_bias: float32 [5120], replicated
- w_up: bfloat16 [5120, 20480], P(None, 'tp')
- b_up: bfloat16 [20480], P('tp')
- w_down: bfloat16 [20480, 5120], P('tp')
- b_down: bfloat16 [5120], replicated
Outputs:
- output: bfloat16 [4, 256, 5120], P('dp', 'tp'), parts along dimension 0
There are 4 independent parts. A program takes and returns all parts, laid end to end along the dimension named above; an argument that names none is the same for every part.
All inputs are finite; a program needn't handle non-finite values.
Results may differ from a plain program's by a relative error of at most 0.010208.
Values are sent between devices in bfloat16 or wider.
A program may use at most 768 MiB of HBM per device.

v0:
```python
import jax
import jax.numpy as jnp
from jax import lax
from jax.sharding import PartitionSpec as P

LN_EPS = 1e-5


def layer_norm(inputs, gain_vec, shift_vec):
    as_f32 = inputs.astype(jnp.float32)
    row_mean = jnp.mean(as_f32, axis=-1, keepdims=True)
    centered = as_f32 - row_mean
    variance = jnp.mean(centered * centered, axis=-1, keepdims=True)
    return (centered * lax.rsqrt(variance + LN_EPS) * gain_vec + shift_vec).astype(jnp.bfloat16)


def causal_attention(queries, keys_all, values):
    seq_len = queries.shape[1]
    head_dim = queries.shape[3]
    logits = jnp.einsum("bqhd,bkhd->bhqk", queries, keys_all, preferred_element_type=jnp.float32) * head_dim ** -0.5
    causal = lax.broadcasted_iota(jnp.int32, (seq_len, seq_len), 0) >= lax.broadcasted_iota(jnp.int32, (seq_len, seq_len), 1)
    logits = jnp.where(causal, logits, -1e30)
    row_max = jnp.max(logits, axis=-1, keepdims=True)
    exp_vals = jnp.exp(logits - row_max)
    weights_bf = (exp_vals / jnp.sum(exp_vals, axis=-1, keepdims=True)).astype(jnp.bfloat16)
    return jnp.einsum("bhqk,bkhd->bqhd", weights_bf, values, preferred_element_type=jnp.float32).astype(jnp.bfloat16)


def solution(mesh):
    group_size = mesh.shape["tp"]

    def scatter_sum(partial):
        n_batch, seq_len, feat_dim = partial.shape
        split_view = partial.astype(jnp.bfloat16).reshape(n_batch, group_size, seq_len // group_size, feat_dim)
        received = lax.all_to_all(split_view, "tp", 1, 1, tiled=True)
        return jnp.sum(received.astype(jnp.float32), axis=1)

    def device_body(hidden, ln1_gain, ln1_bias, w_qkv, b_qkv, w_out, b_out, ln2_gain, ln2_bias, w_up, b_up, w_down, b_down):
        normed = layer_norm(hidden, ln1_gain, ln1_bias)
        normed_all = lax.all_gather(normed, "tp", axis=1, tiled=True)
        qkv_acc = jnp.einsum("bsd,dthe->bsthe", normed_all, w_qkv, preferred_element_type=jnp.float32)
        qkv_all = (qkv_acc + b_qkv.astype(jnp.float32)).astype(jnp.bfloat16)
        context = causal_attention(qkv_all[:, :, 0], qkv_all[:, :, 1], qkv_all[:, :, 2])
        attn_part = jnp.einsum("bqhd,hde->bqe", context, w_out, preferred_element_type=jnp.float32)
        attn_sum = scatter_sum(attn_part)
        resid_mid = (hidden.astype(jnp.float32) + (attn_sum + b_out.astype(jnp.float32))).astype(jnp.bfloat16)
        normed_mid = layer_norm(resid_mid, ln2_gain, ln2_bias)
        mid_all = lax.all_gather(normed_mid, "tp", axis=1, tiled=True)
        up_proj = jnp.einsum("bsd,df->bsf", mid_all, w_up, preferred_element_type=jnp.float32) + b_up.astype(jnp.float32)
        gelu_out = jax.nn.gelu(up_proj, approximate=True).astype(jnp.bfloat16)
        down_part = jnp.einsum("bsf,fd->bsd", gelu_out, w_down, preferred_element_type=jnp.float32)
        down_sum = scatter_sum(down_part)
        return (resid_mid.astype(jnp.float32) + (down_sum + b_down.astype(jnp.float32))).astype(jnp.bfloat16)

    in_layout = (P("dp", "tp", None), P(), P(), P(None, None, "tp", None), P(None, "tp", None), P("tp", None, None), P(), P(), P(), P(None, "tp"), P("tp"), P("tp", None), P())
    layer_fn = jax.shard_map(device_body, mesh=mesh, in_specs=in_layout, out_specs=P("dp", "tp", None), check_vma=False)
    return layer_fn
```

profile of v0, /device:TPU:81, one launch (start us, length us, event | category | flops | bytes accessed | tf_op | source)
XLA Modules:
  0.0 188.3 jit_solution(9874994765218522340)
XLA Ops:
  6.5 0.0 all-gather.3.cloned.1.call-start
  6.6 1.1 convert_reduce_fusion.3
  7.7 1.2 fusion.36
  8.9 1.9 %fusion.39 = bf16[1,32,5120]{2,1,0:T(8,128)(2,1)} fusion(bf16[1,32,5120]{2,1,0:T(8,128)(2,1)} %param.13, f32[5120]{0:T(1024)} %param.15, f32[5120]{0:T(1024)} %param.14, f32[32]{0:T(128)S(1)} %add_rsqrt_fusion.1, f32[32]{0:T(128)S(1)} %broadcast_multiply_fusion.1), kind=kLoop, calls=%fused_computation.50 | loop fusion | flops 983040 | bytes 696576 | tf_op jit(solution)/shard_map/convert_element_type | solution.py:14
  10.8 0.1 all-gather.3.cloned.1.call-update
  10.9 0.7 copy.18
  11.6 26.9 %all-gather.3.cloned.1.call-done = bf16[1,256,5120]{2,1,0:T(8,128)(2,1)} async-done(((bf16[1,32,5120]{2,1,0:T(8,128)(2,1)}), bf16[1,256,5120]{2,1,0:T(8,128)(2,1)}) %all-gather.3.cloned.1.call-update) | async-done | bytes 2621456 | tf_op jit(solution)/shard_map/all_gather | solution.py:40
  38.6 12.8 %fusion.19 = bf16[1,256,3,5,128]{4,1,3,2,0:T(8,128)(2,1)S(1)} fusion(bf16[5120,3,5,128]{3,0,2,1:T(8,128)(2,1)} %param.16, bf16[1,256,5120]{2,1,0:T(8,128)(2,1)} %all-gather.3.cloned.1.call-done, f32[3,5,128]{2,1,0:T(8,128)S(1)} %copy.18), kind=kOutput, calls=%fused_computation.24 | convolution fusion | flops 5034147840 | bytes 23272960 | tf_op jit(solution)/shard_map/bsd,dthe->bsthe/dot_general | solution.py:41
  51.4 0.4 fusion.16
  51.8 0.6 fusion.51
  52.3 7.0 %fusion.1 = bf16[256,5120]{1,0:T(8,128)(2,1)} fusion(bf16[5,128,5120]{2,1,0:T(8,128)(2,1)} %param.18, f32[5,256]{1,0:T(8,128)S(1)} %fusion.51, bf16[1,256,3,5,128]{4,1,3,2,0:T(8,128)(2,1)S(1)} %fusion.19, f32[5,256,256]{1,2,0:T(8,128)S(1)} %fusion.16), kind=kOutput, calls=%fused_computation.2 | convolution fusion | flops 1764066816 | bytes 12132352 | tf_op jit(solution)/shard_map/bqhd,hde->bqe/dot_general | solution.py:44
  59.3 0.0 copy-start.3
  59.3 4.0 %all-to-all-start = ((bf16[1,8,32,5120]{3,2,0,1:T(8,128)(2,1)}), bf16[1,8,32,5120]{3,2,0,1:T(8,128)(2,1)S(1)}, u32[]{:S(2)}, u32[]{:S(2)}) async-start(bf16[1,8,32,5120]{3,2,0,1:T(8,128)(2,1)} %bitcast.67), calls=%async_computation | async-start | bytes 5242880 | tf_op jit(solution)/shard_map/all_to_all | solution.py:35
  63.3 0.0 copy-start
  63.3 0.0 copy-start.1
  63.3 0.0 copy-start.2
  63.3 0.1 all-gather.5.cloned.1.call-start
  63.4 0.0 copy-done.3
  63.4 0.0 copy-start.5
  63.4 31.5 %all-to-all-done = bf16[1,8,32,5120]{3,2,0,1:T(8,128)(2,1)S(1)} async-done(((bf16[1,8,32,5120]{3,2,0,1:T(8,128)(2,1)}), bf16[1,8,32,5120]{3,2,0,1:T(8,128)(2,1)S(1)}, u32[]{:S(2)}, u32[]{:S(2)}) %all-to-all-start) | async-done | bytes 2621472 | tf_op jit(solution)/shard_map/all_to_all | solution.py:35
  94.9 0.4 convert_reduce_fusion.1
  95.3 0.0 copy-done
  95.3 0.2 convert_reduce_fusion.2
  95.6 0.3 fusion.32
  95.9 0.0 copy-done.1
  95.9 0.0 copy-done.2
  95.9 0.9 fusion.35
  96.8 0.1 all-gather.5.cloned.1.call-update
  96.9 0.0 copy-done.5
  96.9 23.4 %all-gather.5.cloned.1.call-done = bf16[1,256,5120]{2,1,0:T(8,128)(2,1)} async-done(((bf16[1,32,5120]{2,1,0:T(8,128)(2,1)}), bf16[1,256,5120]{2,1,0:T(8,128)(2,1)}) %all-gather.5.cloned.1.call-update) | async-done | bytes 2621456 | tf_op jit(solution)/shard_map/all_gather | solution.py:48
  120.2 24.3 %convolution_convert_fusion = bf16[256,5120]{1,0:T(8,128)(2,1)} fusion(bf16[2560,5120]{1,0:T(8,128)(2,1)} %param.24, bf16[5120,2560]{1,0:T(8,128)(2,1)} %param.22, bf16[1,256,5120]{2,1,0:T(8,128)(2,1)} %all-gather.5.cloned.1.call-done, f32[2560]{0:T(1024)S(1)} %convert_element_type.84), kind=kOutput, calls=%fused_computation.3 | convolution fusion | flops 13429637120 | bytes 57681920 | tf_op jit(solution)/shard_map/bsf,fd->bsd/dot_general | solution.py:51
  144.6 0.0 copy-start.4
  144.6 4.0 %all-to-all-start.1 = ((bf16[1,8,32,5120]{3,2,0,1:T(8,128)(2,1)}), bf16[1,8,32,5120]{3,2,0,1:T(8,128)(2,1)S(1)}, u32[]{:S(2)}, u32[]{:S(2)}) async-start(bf16[1,8,32,5120]{3,2,0,1:T(8,128)(2,1)} %bitcast.68), calls=%async_computation.1 | async-start | bytes 5242880 | tf_op jit(solution)/shard_map/all_to_all | solution.py:35
  148.6 0.0 copy-done.4
  148.6 31.7 %all-to-all-done.1 = bf16[1,8,32,5120]{3,2,0,1:T(8,128)(2,1)S(1)} async-done(((bf16[1,8,32,5120]{3,2,0,1:T(8,128)(2,1)}), bf16[1,8,32,5120]{3,2,0,1:T(8,128)(2,1)S(1)}, u32[]{:S(2)}, u32[]{:S(2)}) %all-to-all-start.1) | async-done | bytes 2621472 | tf_op jit(solution)/shard_map/all_to_all | solution.py:35
  180.2 0.4 convert_reduce_fusion
  180.6 0.8 fusion.41
  (8 shorter events, 0.1 us)
Async XLA Ops:
  6.5 32.0 %all-gather.3.cloned.1.call-start = ((), (), s32[]{:S(2)}) async-start(), calls=%async_computation.2 | async-start | bytes 2949120 | tf_op jit(solution)/shard_map/all_gather | solution.py:40
  59.3 4.1 %copy-start.3 = (bf16[5120]{0:T(1024)(128)(2,1)S(1)}, bf16[5120]{0:T(1024)(128)(2,1)}, u32[]{:S(2)}) copy-start(bf16[5120]{0:T(1024)(128)(2,1)} %param.19) | copy-start | bytes 30724
  59.3 35.7 %all-to-all-start = ((bf16[1,8,32,5120]{3,2,0,1:T(8,128)(2,1)}), bf16[1,8,32,5120]{3,2,0,1:T(8,128)(2,1)S(1)}, u32[]{:S(2)}, u32[]{:S(2)}) async-start(bf16[1,8,32,5120]{3,2,0,1:T(8,128)(2,1)} %bitcast.67), calls=%async_computation | async-start | bytes 5242880 | tf_op jit(solution)/shard_map/all_to_all | solution.py:35
  63.3 32.0 %copy-start = (bf16[1,32,5120]{2,1,0:T(8,128)(2,1)S(1)}, bf16[1,32,5120]{2,1,0:T(8,128)(2,1)}, u32[]{:S(2)}) copy-start(bf16[1,32,5120]{2,1,0:T(8,128)(2,1)} %param.13) | copy-start | bytes 983044
  63.3 32.6 %copy-start.1 = (f32[5120]{0:T(1024)S(1)}, f32[5120]{0:T(1024)}, u32[]{:S(2)}) copy-start(f32[5120]{0:T(1024)} %param.21) | copy-start | bytes 61444
  63.3 32.6 %copy-start.2 = (f32[5120]{0:T(1024)S(1)}, f32[5120]{0:T(1024)}, u32[]{:S(2)}) copy-start(f32[5120]{0:T(1024)} %param.20) | copy-start | bytes 61444
  63.3 57.0 %all-gather.5.cloned.1.call-start = ((), (), s32[]{:S(2)}) async-start(), calls=%async_computation.3 | async-start | bytes 2949120 | tf_op jit(solution)/shard_map/all_gather | solution.py:48
  63.4 33.5 %copy-start.5 = (bf16[2560]{0:T(1024)(128)(2,1)S(1)}, bf16[2560]{0:T(1024)(128)(2,1)}, u32[]{:S(2)}) copy-start(bf16[2560]{0:T(1024)(128)(2,1)} %param.23) | copy-start | bytes 15364
  144.6 4.0 %copy-start.4 = (bf16[5120]{0:T(1024)(128)(2,1)S(1)}, bf16[5120]{0:T(1024)(128)(2,1)}, u32[]{:S(2)}) copy-start(bf16[5120]{0:T(1024)(128)(2,1)} %param.25) | copy-start | bytes 30724
  144.6 35.7 %all-to-all-start.1 = ((bf16[1,8,32,5120]{3,2,0,1:T(8,128)(2,1)}), bf16[1,8,32,5120]{3,2,0,1:T(8,128)(2,1)S(1)}, u32[]{:S(2)}, u32[]{:S(2)}) async-start(bf16[1,8,32,5120]{3,2,0,1:T(8,128)(2,1)} %bitcast.68), calls=%async_computation.1 | async-start | bytes 5242880 | tf_op jit(solution)/shard_map/all_to_all | solution.py:35
Sparse Core Ops, SparseCore 0:
  11.0 27.4 all-gather.2
  97.0 23.2 all-gather.4
where the time goes:
time: 189 us; the launch traced here: 188 us
  waiting for transfers between devices  114 us (60%)
  matrix products  45 us (24%)
  between operations  13.5 us (7%)
  starting transfers between devices  8.07 us (4%)
  other arithmetic  7.34 us (4%)
    all_to_all x2, waiting for transfers between devices, scatter_sum(): received = lax.all_to_all(split_view, 'tp', 1, 1, tiled=True)  63.2 us
    all_gather x1, waiting for transfers between devices, device_body(): normed_all = lax.all_gather(normed, 'tp', axis=1, tiled=True)  26.9 us
    dot_general x1, matrix products, device_body(): jnp.einsum('bsf,fd->bsd', gelu_out, w_down, preferred_element_type=jnp.fl...  24.3 us
    all_gather x1, waiting for transfers between devices, device_body(): mid_all = lax.all_gather(normed_mid, 'tp', axis=1, tiled=True)  23.4 us
    dot_general x1, matrix products, device_body(): jnp.einsum('bsd,dthe->bsthe', normed_all, w_qkv, preferred_element_type=j...  12.8 us
    all_to_all x2, starting transfers between devices, scatter_sum(): received = lax.all_to_all(split_view, 'tp', 1, 1, tiled=True)  8 us
    dot_general x1, matrix products, device_body(): jnp.einsum('bqhd,hde->bqe', context, w_out, preferred_element_type=jnp.fl...  6.97 us
  transfers between devices with their start and end apart: 4, of which 4 were waited for; matrix products, arithmetic and copies ran while one was open for 0% of the time, Pallas kernels for 0%

commit v1 on v0

v1 whole, which is shorter than its diff:
```python
import functools

import jax
import jax.numpy as jnp
from jax import lax
from jax.experimental import pallas as pl
from jax.experimental.pallas import tpu as pltpu
from jax.sharding import PartitionSpec as P

LN_EPS = 1e-5
MESH = pl.DeviceIdType.MESH
CH = 512
LOOK = 4
LAG_B, LAG_C = 2, 3
LAG_P, LAG_H, LAG_F = 1, 3, 5
N_WD = 6


def f32(v):
    return v.astype(jnp.float32)


def dot(a, b):
    return jnp.dot(a, b, preferred_element_type=jnp.float32)


def layer_kernel(
    n_dev,
    x_ref, g1_ref, s1_ref, wqkv, bqkv_ref, wo, bo_ref, g2_ref, s2_ref, wu, bu_ref, wd, bd_ref,
    out_ref,
    h_all, u_w, d_w, o_w, acc, qkv, ctx, act, psend, precv,
    hop_s, hop_r, fin_s, fin_r, x1,
    usem, osem, dsem, ag_send, ag_l, ag_r, ag_l2, ag_r2, ag_p,
    rs_send, rs_p, rs_hl, rs_hr, rs_fl, rs_fr,
):
    n_chips = n_dev // 2
    rows, dim = x_ref.shape
    nch = dim // CH
    half = rows // 2
    side = rows * n_chips
    n_tok = 2 * side
    n_slab = wqkv.shape[0]
    hd = wqkv.shape[2]
    heads = n_slab // 3
    qw = n_slab * hd
    ff = wu.shape[1]
    me = lax.axis_index("tp")
    chip, core = me // 2, me % 2
    right = {"tp": ((chip + 1) % n_chips) * 2 + core}
    left = {"tp": ((chip + n_chips - 1) % n_chips) * 2 + core}
    mate = {"tp": chip * 2 + (1 - core)}

    def push(src, dst, ssem, rsem, dev):
        return pltpu.make_async_remote_copy(
            src_ref=src, dst_ref=dst, send_sem=ssem, recv_sem=rsem, device_id=dev, device_id_type=MESH)

    barrier = pltpu.get_barrier_semaphore()
    for dev in (left, right, mate):
        pl.semaphore_signal(barrier, inc=1, device_id=dev, device_id_type=MESH)

    def load_qkv(j):
        for s in range(n_slab):
            pltpu.make_async_copy(
                wqkv.at[s, pl.ds(pl.multiple_of(j * CH, CH), CH), :],
                u_w.at[j, :, pl.ds(s * hd, hd)], usem.at[j]).start()

    def load_up(j):
        return pltpu.make_async_copy(
            wu.at[pl.ds(pl.multiple_of(j * CH, CH), CH), :], u_w.at[j], usem.at[j])

    def load_down(j):
        slot = j % N_WD
        return pltpu.make_async_copy(
            wd.at[:, pl.ds(pl.multiple_of(j * CH, CH), CH)], d_w.at[slot], dsem.at[slot])

    def init_loads(j, c):
        load_qkv(j)
        return c

    lax.fori_loop(0, nch, init_loads, 0)
    out_load = pltpu.make_async_copy(wo, o_w, osem)
    out_load.start()
    for j in range(N_WD):
        load_down(j).start()

    def norm(get, gain_ref, shift_ref):
        tot = jnp.zeros((rows, CH), jnp.float32)
        for j in range(nch):
            tot += get(j)
        mean = jnp.sum(tot, axis=1, keepdims=True) * (1.0 / dim)
        tot = jnp.zeros((rows, CH), jnp.float32)
        for j in range(nch):
            cen = get(j) - mean
            tot += cen * cen
        var = jnp.sum(tot, axis=1, keepdims=True) * (1.0 / dim)
        inv = lax.rsqrt(var + LN_EPS)
        for j in range(nch):
            cols = slice(j * CH, (j + 1) * CH)
            y = (get(j) - mean) * inv * gain_ref[:, cols] + shift_ref[:, cols]
            h_all[j, 0:rows, :] = y.astype(jnp.bfloat16)

    norm(lambda j: f32(x_ref[:, j * CH:(j + 1) * CH]), g1_ref, s1_ref)
    acc[...] = jnp.zeros_like(acc)
    pl.semaphore_wait(barrier, 3)

    def at(j, s, r, lo=0, n=rows):
        return h_all.at[j, pl.ds(s * side + r * rows + lo, n), :]

    def gather(consume):
        def own(j):
            push(at(j, 0, 0), at(j, 0, n_chips - 1), ag_send, ag_l.at[j], right).start()
            push(at(j, 0, 0), at(j, 0, 1), ag_send, ag_r.at[j], left).start()
            push(at(j, 0, 0), at(j, 1, 0), ag_send, ag_p.at[j], mate).start()

        for j in range(LOOK):
            own(j)

        def step(i, c):
            @pl.when(i + LOOK < nch)
            def _():
                own(i + LOOK)

            @pl.when(i < nch)
            def _():
                push(at(i, 0, 0), at(i, 0, 3), ag_send, ag_l.at[i], right).wait_recv()
                push(at(i, 0, 3, 0, half), at(i, 0, 2, 0, half), ag_send, ag_l2.at[i], right).start()
                push(at(i, 0, 3), at(i, 1, 3), ag_send, ag_p.at[i], mate).start()
                push(at(i, 0, 0), at(i, 0, 1), ag_send, ag_r.at[i], left).wait_recv()
                push(at(i, 0, 1, half, half), at(i, 0, 2, half, half), ag_send, ag_r2.at[i], left).start()
                push(at(i, 0, 1), at(i, 1, 1), ag_send, ag_p.at[i], mate).start()

            @pl.when((i >= LAG_B) & (i < nch + LAG_B))
            def _():
                j = i - LAG_B
                push(at(j, 0, 3, 0, half), at(j, 0, 2, 0, half), ag_send, ag_l2.at[j], right).wait_recv()
                push(at(j, 0, 1, half, half), at(j, 0, 2, half, half), ag_send, ag_r2.at[j], left).wait_recv()
                push(at(j, 0, 2), at(j, 1, 2), ag_send, ag_p.at[j], mate).start()

            @pl.when(i >= LAG_C)
            def _():
                j = i - LAG_C
                push(at(j, 0, 0, 0, side), at(j, 1, 0, 0, side), ag_send, ag_p.at[j], mate).wait_recv()
                consume(j)
            return c

        lax.fori_loop(0, nch + LAG_C, step, 0)

    def gather_drain():
        sent = h_all.at[:, pl.ds(0, 7 * rows), :]
        push(sent, sent, ag_send, ag_p.at[0], mate).wait_send()

    def own_part(j, r, lo=0, n=rows):
        return acc.at[j // 2, pl.ds((j % 2) * side + r * rows + lo, n), :]

    def scatter(partial, finish):
        def step(i, c):
            @pl.when(i < nch)
            def _():
                p = partial(i)
                acc[i // 2, pl.ds(pl.multiple_of((i % 2) * side, side), side), :] = p[0:side]
                psend[i] = p[side:].astype(jnp.bfloat16)
                push(psend.at[i], precv.at[i], rs_send, rs_p.at[i], mate).start()

            @pl.when((i >= LAG_P) & (i < nch + LAG_P))
            def _():
                j = i - LAG_P
                base = pl.multiple_of((j % 2) * side, side)
                push(psend.at[j], precv.at[j], rs_send, rs_p.at[j], mate).wait_recv()
                s = acc[j // 2, pl.ds(base, side), :] + f32(precv[j])
                hop_s[0, j] = s[2 * rows:2 * rows + half].astype(jnp.bfloat16)
                hop_s[1, j] = s[2 * rows + half:3 * rows].astype(jnp.bfloat16)
                push(hop_s.at[0, j], hop_r.at[0, j], rs_send, rs_hl.at[j], right).start()
                push(hop_s.at[1, j], hop_r.at[1, j], rs_send, rs_hr.at[j], left).start()
                acc[j // 2, pl.ds(base, side), :] = s

            @pl.when((i >= LAG_H) & (i < nch + LAG_H))
            def _():
                j = i - LAG_H
                base = pl.multiple_of((j % 2) * side, side)
                push(hop_s.at[0, j], hop_r.at[0, j], rs_send, rs_hl.at[j], right).wait_recv()
                one = acc[j // 2, pl.ds(base + rows, rows), :]
                fin_s[0, j, 0:half] = (one[0:half] + f32(hop_r[0, j])).astype(jnp.bfloat16)
                fin_s[0, j, half:] = one[half:].astype(jnp.bfloat16)
                push(fin_s.at[0, j], fin_r.at[0, j], rs_send, rs_fl.at[j], right).start()
                push(hop_s.at[1, j], hop_r.at[1, j], rs_send, rs_hr.at[j], left).wait_recv()
                three = acc[j // 2, pl.ds(base + 3 * rows, rows), :]
                fin_s[1, j, 0:half] = three[0:half].astype(jnp.bfloat16)
                fin_s[1, j, half:] = (three[half:] + f32(hop_r[1, j])).astype(jnp.bfloat16)
                push(fin_s.at[1, j], fin_r.at[1, j], rs_send, rs_fr.at[j], left).start()

            @pl.when(i >= LAG_F)
            def _():
                j = i - LAG_F
                base = pl.multiple_of((j % 2) * side, side)
                push(fin_s.at[0, j], fin_r.at[0, j], rs_send, rs_fl.at[j], right).wait_recv()
                push(fin_s.at[1, j], fin_r.at[1, j], rs_send, rs_fr.at[j], left).wait_recv()
                finish(j, acc[j // 2, pl.ds(base, rows), :] + f32(fin_r[0, j]) + f32(fin_r[1, j]))
            return c

        lax.fori_loop(0, nch + LAG_F, step, 0)

    def scatter_drain():
        push(psend, precv, rs_send, rs_p.at[0], mate).wait_send()
        push(hop_s, hop_r, rs_send, rs_p.at[0], mate).wait_send()
        push(fin_s, fin_r, rs_send, rs_p.at[0], mate).wait_send()

    tiles = [(t, min(CH, qw - t * CH)) for t in range((qw + CH - 1) // CH)]

    def use_qkv(j):
        pltpu.make_async_copy(u_w.at[j, :, pl.ds(0, qw)], u_w.at[j, :, pl.ds(0, qw)], usem.at[j]).wait()
        for t, n in tiles:
            acc[t, :, 0:n] += dot(h_all[j], u_w[j, :, t * CH:t * CH + n])
        load_up(j).start()

    gather(use_qkv)
    for t, n in tiles:
        cols = slice(t * CH, t * CH + n)
        qkv[:, cols] = (acc[t, :, 0:n] + f32(bqkv_ref[:, cols])).astype(jnp.bfloat16)

    def position(i):
        s, r, w = i // side, (i // rows) % n_chips, i % rows
        return ((chip + r) % n_chips) * (2 * rows) + (core + s - 2 * core * s) * rows + w

    qpos = position(lax.broadcasted_iota(jnp.int32, (n_tok, n_tok), 0))
    kpos = position(lax.broadcasted_iota(jnp.int32, (n_tok, n_tok), 1))
    keep = qpos >= kpos
    for h in range(heads):
        q = qkv[:, h * hd:(h + 1) * hd]
        k = qkv[:, (heads + h) * hd:(heads + h + 1) * hd]
        v = qkv[:, (2 * heads + h) * hd:(2 * heads + h + 1) * hd]
        logits = lax.dot_general(q, k, (((1,), (1,)), ((), ())), preferred_element_type=jnp.float32) * hd ** -0.5
        logits = jnp.where(keep, logits, -1e30)
        e = jnp.exp(logits - jnp.max(logits, axis=1, keepdims=True))
        p = (e / jnp.sum(e, axis=1, keepdims=True)).astype(jnp.bfloat16)
        ctx[:, h * hd:(h + 1) * hd] = dot(p, v).astype(jnp.bfloat16)

    gather_drain()
    out_load.wait()

    def out_part(j):
        return dot(ctx[...], o_w[:, pl.ds(pl.multiple_of(j * CH, CH), CH)])

    def out_finish(j, total):
        cols = pl.ds(pl.multiple_of(j * CH, CH), CH)
        x1[j] = (f32(x_ref[:, cols]) + (total + f32(bo_ref[:, cols]))).astype(jnp.bfloat16)

    scatter(out_part, out_finish)

    norm(lambda j: f32(x1[j]), g2_ref, s2_ref)
    acc[...] = jnp.zeros_like(acc)

    def use_up(j):
        load_up(j).wait()
        for t in range(ff // CH):
            acc[t] += dot(h_all[j], u_w[j, :, t * CH:(t + 1) * CH])

    gather(use_up)
    for t in range(ff // CH):
        cols = slice(t * CH, (t + 1) * CH)
        a = acc[t] + f32(bu_ref[:, cols])
        act[:, cols] = jax.nn.gelu(a, approximate=True).astype(jnp.bfloat16)
    scatter_drain()
    gather_drain()

    def down_part(j):
        load_down(j).wait()
        p = dot(act[...], d_w[j % N_WD])

        @pl.when(j + N_WD < nch)
        def _():
            load_down(j + N_WD).start()
        return p

    def down_finish(j, total):
        cols = pl.ds(pl.multiple_of(j * CH, CH), CH)
        out_ref[:, cols] = (f32(x1[j]) + (total + f32(bd_ref[:, cols]))).astype(jnp.bfloat16)

    scatter(down_part, down_finish)
    scatter_drain()


def solution(mesh):
    n_dev = mesh.shape["tp"]

    def body(hidden, g1, s1, w_qkv, b_qkv, w_out, b_out, g2, s2, w_up, b_up, w_down, b_down):
        _, rows, dim = hidden.shape
        _, three, heads, hd = w_qkv.shape
        ff = w_up.shape[1]
        nch = dim // CH
        n_tok, side, half = rows * n_dev, rows * n_dev // 2, rows // 2
        bf, fl = jnp.bfloat16, jnp.float32
        row = lambda v: v.reshape(1, -1)
        vmem = pl.BlockSpec(memory_space=pltpu.VMEM)
        hbm = pl.BlockSpec(memory_space=pl.ANY)
        dma = pltpu.SemaphoreType.DMA
        out = pl.pallas_call(
            functools.partial(layer_kernel, n_dev),
            out_shape=jax.ShapeDtypeStruct((rows, dim), bf),
            in_specs=[vmem, vmem, vmem, hbm, vmem, hbm, vmem, vmem, vmem, hbm, vmem, hbm, vmem],
            out_specs=vmem,
            scratch_shapes=[
                pltpu.VMEM((nch, n_tok, CH), bf),
                pltpu.VMEM((nch, CH, ff), bf),
                pltpu.VMEM((N_WD, ff, CH), bf),
                pltpu.VMEM((heads * hd, dim), bf),
                pltpu.VMEM((nch // 2, n_tok, CH), fl),
                pltpu.VMEM((n_tok, three * heads * hd), bf),
                pltpu.VMEM((n_tok, heads * hd), bf),
                pltpu.VMEM((n_tok, ff), bf),
                pltpu.VMEM((nch, side, CH), bf),
                pltpu.VMEM((nch, side, CH), bf),
                pltpu.VMEM((2, nch, half, CH), bf),
                pltpu.VMEM((2, nch, half, CH), bf),
                pltpu.VMEM((2, nch, rows, CH), bf),
                pltpu.VMEM((2, nch, rows, CH), bf),
                pltpu.VMEM((nch, rows, CH), bf),
                dma((nch,)), dma(()), dma((N_WD,)),
                dma(()), dma((nch,)), dma((nch,)), dma((nch,)), dma((nch,)), dma((nch,)),
                dma(()), dma((nch,)), dma((nch,)), dma((nch,)), dma((nch,)), dma((nch,)),
            ],
            compiler_params=pltpu.CompilerParams(
                collective_id=0, has_side_effects=True, vmem_limit_bytes=67043328),
            name="decoder_layer",
        )(
            hidden[0], row(g1), row(s1),
            jnp.transpose(w_qkv, (1, 2, 0, 3)).reshape(three * heads, dim, hd), row(b_qkv),
            w_out.reshape(heads * hd, dim), row(b_out), row(g2), row(s2), w_up, row(b_up), w_down, row(b_down),
        )
        return out[None]

    specs = (P("dp", "tp", None), P(), P(), P(None, None, "tp", None), P(None, "tp", None),
             P("tp", None, None), P(), P(), P(), P(None, "tp"), P("tp"), P("tp", None), P())
    return jax.shard_map(body, mesh=mesh, in_specs=specs, out_specs=P("dp", "tp", None), check_vma=False)
```

time: 189 us -> 99.7 us (0.53)
  waiting for transfers between devices: 114 us -> 0 us
  Pallas kernels: 0 us -> 92.3 us
  matrix products: 45 us -> 0 us
  between operations: 13.5 us -> 0.01 us
  starting transfers between devices: 8.07 us -> 0 us
  other arithmetic: 7.34 us -> 0 us
  local copies, waits for them, and re-layouts: 0.72 us -> 6.96 us
    pallas_call x0 -> x1, Pallas kernels: none -> 92.3 us  [body(): pl.pallas_call(functools.partial(layer_kernel, n_dev), out_shape=jax.Shap...]
    all_to_all x2 -> x0, waiting for transfers between devices: 63.2 us -> none  [scatter_sum(): received = lax.all_to_all(split_view, 'tp', 1, 1, tiled=True)]
    all_gather x2 -> x0, waiting for transfers between devices: 50.3 us -> none  [the longest x1 26.9 us: device_body(): normed_all = lax.all_gather(normed, 'tp', axis=1, tiled=True)]
    dot_general x4 -> x0, matrix products: 44.5 us -> none  [the longest x1 24.3 us: device_body(): jnp.einsum('bsf,fd->bsd', gelu_out, w_down, preferred_element_type=jnp.fl...]
    all_to_all x2 -> x0, starting transfers between devices: 8 us -> none  [scatter_sum(): received = lax.all_to_all(split_view, 'tp', 1, 1, tiled=True)]
    reshape x0 -> x4, local copies, waits for them, and re-layouts: none -> 4.55 us  [body(): row = lambda v: v.reshape(1, -1)]
    convert_element_type x6 -> x0, other arithmetic: 3.66 us -> none  [the longest x2 2.82 us: layer_norm(): (centered * lax.rsqrt(variance + LN_EPS) * gain_vec + shift_vec).astype(j...]
    reduce_sum x6 -> x0, other arithmetic: 3.62 us -> none  [the longest x2 1.51 us: layer_norm(): variance = jnp.mean(centered * centered, axis=-1, keepdims=True)]
  transfers between devices with their start and end apart: 4 -> 0, of which waited for: 4 -> 0; matrix products, arithmetic and copies ran while one was open for 0% -> 0% of each run, Pallas kernels for 0% -> 0%
where the time goes in v1:
time: 99.7 us; the launch traced here: 99.3 us
  Pallas kernels  92.3 us (93%)
  local copies, waits for them, and re-layouts  6.96 us (7%)
    pallas_call x1, Pallas kernels, body(): pl.pallas_call(functools.partial(layer_kernel, n_dev), out_shape=jax.Shap...  92.3 us
    reshape x4, local copies, waits for them, and re-layouts, body(): row = lambda v: v.reshape(1, -1)  4.55 us
    unnamed x2, local copies, waits for them, and re-layouts  2.41 us

profile of v1, /device:TPU:81, one launch (start us, length us, event | category | flops | bytes accessed | tf_op | source)
XLA Modules:
  0.0 99.3 jit_solution(4646267687273526785)
XLA Ops:
  0.0 0.7 copy.15
  0.7 0.6 reshape.33.bqkv_ref
  1.3 1.3 %reshape.38.bu_ref = bf16[1,2560]{1,0:T(2,128)(2,1)} reshape(bf16[2560]{0:T(1024)(128)(2,1)} %param.23) | data formatting | bytes 10240 | tf_op jit(solution)/shard_map/reshape | solution.py:292
  2.6 1.3 %reshape.35.bo_ref = bf16[1,5120]{1,0:T(2,128)(2,1)} reshape(bf16[5120]{0:T(1024)(128)(2,1)} %param.19) | data formatting | bytes 20480 | tf_op jit(solution)/shard_map/reshape | solution.py:292
  3.9 1.3 %reshape.39.bd_ref = bf16[1,5120]{1,0:T(2,128)(2,1)} reshape(bf16[5120]{0:T(1024)(128)(2,1)} %param.25) | data formatting | bytes 20480 | tf_op jit(solution)/shard_map/reshape | solution.py:292
  5.2 92.3 %decoder_layer.1 = bf16[32,5120]{1,0:T(8,128)(2,1)} custom-call(bf16[32,5120]{1,0:T(8,128)(2,1)} %bitcast.13, f32[1,5120]{1,0:T(1,128)} %bitcast.14, f32[1,5120]{1,0:T(1,128)} %bitcast.15, bf16[15,5120,128]{2,1,0:T(8,128)(2,1)} %bitcast.10, bf16[1,1920]{1,0:T(2,128)(2,1)} %reshape.33.bqkv_ref, bf16[640,5120]{1,0:T(8,128)(2,1)} %bitcast.11, ...), custom_call_target="tpu_custom_call" | custom-call | tf_op jit(solution)/shard_map/decoder_layer/pallas_call | solution.py:296
  97.6 1.7 %copy.17 = bf16[1,32,5120]{2,1,0:T(8,128)(2,1)} copy(bf16[1,32,5120]{2,1,0:T(8,128)(2,1)} %bitcast.12) | data formatting | bytes 655360

commit v2 on v1

--- a/solution.py
+++ b/solution.py
@@ -10,9 +10,10 @@
 LN_EPS = 1e-5
 MESH = pl.DeviceIdType.MESH
 CH = 512
-LOOK = 4
-LAG_B, LAG_C = 2, 3
-LAG_P, LAG_H, LAG_F = 1, 3, 5
+LOOK = 5
+LAG_B, LAG_C = 5, 6
+LAGS_OUT = (2, 8, 12)
+LAGS_DOWN = (2, 5, 9)
 N_WD = 6
 
 
@@ -26,13 +27,20 @@
 
 def layer_kernel(
     n_dev,
-    x_ref, g1_ref, s1_ref, wqkv, bqkv_ref, wo, bo_ref, g2_ref, s2_ref, wu, bu_ref, wd, bd_ref,
-    out_ref,
-    h_all, u_w, d_w, o_w, acc, qkv, ctx, act, psend, precv,
+    x_hbm, g1_hbm, s1_hbm, wqkv, bqkv_hbm, wo, bo_hbm, g2_hbm, s2_hbm, wu, bu_hbm, wd, bd_hbm,
+    out_hbm,
+    x_ref, g1_ref, s1_ref, g2_ref, s2_ref, bqkv_ref, bo_ref, bu_ref, bd_ref,
+    xb, h_all, u_w, d_w, o_w, acc, qkv, ctx, act, psend, precv,
     hop_s, hop_r, fin_s, fin_r, x1,
-    usem, osem, dsem, ag_send, ag_l, ag_r, ag_l2, ag_r2, ag_p,
+    xsem, psem, usem, osem, dsem, outsem, ag_send, ag_l, ag_r, ag_l2, ag_r2, ag_p,
     rs_send, rs_p, rs_hl, rs_hr, rs_fl, rs_fr,
 ):
+    small = [pltpu.make_async_copy(a, b, xsem.at[i]) for i, (a, b) in enumerate(
+        ((x_hbm, x_ref), (g1_hbm, g1_ref), (s1_hbm, s1_ref)))]
+    late = [pltpu.make_async_copy(a, b, psem.at[i]) for i, (a, b) in enumerate(
+        ((bqkv_hbm, bqkv_ref), (bo_hbm, bo_ref), (g2_hbm, g2_ref), (s2_hbm, s2_ref), (bu_hbm, bu_ref), (bd_hbm, bd_ref)))]
+    for copy in small:
+        copy.start()
     n_chips = n_dev // 2
     rows, dim = x_ref.shape
     nch = dim // CH
@@ -78,6 +86,8 @@
         return c
 
     lax.fori_loop(0, nch, init_loads, 0)
+    for copy in late:
+        copy.start()
     out_load = pltpu.make_async_copy(wo, o_w, osem)
     out_load.start()
     for j in range(N_WD):
@@ -99,6 +109,8 @@
             y = (get(j) - mean) * inv * gain_ref[:, cols] + shift_ref[:, cols]
             h_all[j, 0:rows, :] = y.astype(jnp.bfloat16)
 
+    for copy in small:
+        copy.wait()
     norm(lambda j: f32(x_ref[:, j * CH:(j + 1) * CH]), g1_ref, s1_ref)
     acc[...] = jnp.zeros_like(acc)
     pl.semaphore_wait(barrier, 3)
@@ -152,7 +164,9 @@
     def own_part(j, r, lo=0, n=rows):
         return acc.at[j // 2, pl.ds((j % 2) * side + r * rows + lo, n), :]
 
-    def scatter(partial, finish):
+    def scatter(partial, finish, lags):
+        lag_p, lag_h, lag_f = lags
+
         def step(i, c):
             @pl.when(i < nch)
             def _():
@@ -161,9 +175,9 @@
                 psend[i] = p[side:].astype(jnp.bfloat16)
                 push(psend.at[i], precv.at[i], rs_send, rs_p.at[i], mate).start()
 
-            @pl.when((i >= LAG_P) & (i < nch + LAG_P))
-            def _():
-                j = i - LAG_P
+            @pl.when((i >= lag_p) & (i < nch + lag_p))
+            def _():
+                j = i - lag_p
                 base = pl.multiple_of((j % 2) * side, side)
                 push(psend.at[j], precv.at[j], rs_send, rs_p.at[j], mate).wait_recv()
                 s = acc[j // 2, pl.ds(base, side), :] + f32(precv[j])
@@ -173,9 +187,9 @@
                 push(hop_s.at[1, j], hop_r.at[1, j], rs_send, rs_hr.at[j], left).start()
                 acc[j // 2, pl.ds(base, side), :] = s
 
-            @pl.when((i >= LAG_H) & (i < nch + LAG_H))
-            def _():
-                j = i - LAG_H
+            @pl.when((i >= lag_h) & (i < nch + lag_h))
+            def _():
+                j = i - lag_h
                 base = pl.multiple_of((j % 2) * side, side)
                 push(hop_s.at[0, j], hop_r.at[0, j], rs_send, rs_hl.at[j], right).wait_recv()
                 one = acc[j // 2, pl.ds(base + rows, rows), :]
@@ -188,16 +202,16 @@
                 fin_s[1, j, half:] = (three[half:] + f32(hop_r[1, j])).astype(jnp.bfloat16)
                 push(fin_s.at[1, j], fin_r.at[1, j], rs_send, rs_fr.at[j], left).start()
 
-            @pl.when(i >= LAG_F)
-            def _():
-                j = i - LAG_F
+            @pl.when(i >= lag_f)
+            def _():
+                j = i - lag_f
                 base = pl.multiple_of((j % 2) * side, side)
                 push(fin_s.at[0, j], fin_r.at[0, j], rs_send, rs_fl.at[j], right).wait_recv()
                 push(fin_s.at[1, j], fin_r.at[1, j], rs_send, rs_fr.at[j], left).wait_recv()
                 finish(j, acc[j // 2, pl.ds(base, rows), :] + f32(fin_r[0, j]) + f32(fin_r[1, j]))
             return c
 
-        lax.fori_loop(0, nch + LAG_F, step, 0)
+        lax.fori_loop(0, nch + lag_f, step, 0)
 
     def scatter_drain():
         push(psend, precv, rs_send, rs_p.at[0], mate).wait_send()
@@ -213,9 +227,12 @@
         load_up(j).start()
 
     gather(use_qkv)
-    for t, n in tiles:
-        cols = slice(t * CH, t * CH + n)
-        qkv[:, cols] = (acc[t, :, 0:n] + f32(bqkv_ref[:, cols])).astype(jnp.bfloat16)
+    for copy in late:
+        copy.wait()
+    for s in range(n_slab):
+        lo = s * hd
+        part = acc[lo // CH, :, lo % CH:lo % CH + hd]
+        qkv[:, lo:lo + hd] = (part + f32(bqkv_ref[s % heads, s // heads:s // heads + 1, :])).astype(jnp.bfloat16)
 
     def position(i):
         s, r, w = i // side, (i // rows) % n_chips, i % rows
@@ -237,14 +254,18 @@
     gather_drain()
     out_load.wait()
 
+    bo = f32(bo_ref[...]).reshape(1, dim)
+    for j in range(nch):
+        cols = slice(j * CH, (j + 1) * CH)
+        xb[j] = f32(x_ref[:, cols]) + bo[:, cols]
+
     def out_part(j):
         return dot(ctx[...], o_w[:, pl.ds(pl.multiple_of(j * CH, CH), CH)])
 
     def out_finish(j, total):
-        cols = pl.ds(pl.multiple_of(j * CH, CH), CH)
-        x1[j] = (f32(x_ref[:, cols]) + (total + f32(bo_ref[:, cols]))).astype(jnp.bfloat16)
-
-    scatter(out_part, out_finish)
+        x1[j] = (xb[j] + total).astype(jnp.bfloat16)
+
+    scatter(out_part, out_finish, LAGS_OUT)
 
     norm(lambda j: f32(x1[j]), g2_ref, s2_ref)
     acc[...] = jnp.zeros_like(acc)
@@ -255,12 +276,17 @@
             acc[t] += dot(h_all[j], u_w[j, :, t * CH:(t + 1) * CH])
 
     gather(use_up)
+    bu = f32(bu_ref[...]).reshape(1, ff)
     for t in range(ff // CH):
         cols = slice(t * CH, (t + 1) * CH)
-        a = acc[t] + f32(bu_ref[:, cols])
+        a = acc[t] + bu[:, cols]
         act[:, cols] = jax.nn.gelu(a, approximate=True).astype(jnp.bfloat16)
     scatter_drain()
     gather_drain()
+
+    bd = f32(bd_ref[...]).reshape(1, dim)
+    for j in range(nch):
+        xb[j] = f32(x1[j]) + bd[:, j * CH:(j + 1) * CH]
 
     def down_part(j):
         load_down(j).wait()
@@ -271,12 +297,17 @@
             load_down(j + N_WD).start()
         return p
 
+    def store(j):
+        return pltpu.make_async_copy(x1.at[j], out_hbm.at[:, pl.ds(pl.multiple_of(j * CH, CH), CH)], outsem.at[j])
+
     def down_finish(j, total):
-        cols = pl.ds(pl.multiple_of(j * CH, CH), CH)
-        out_ref[:, cols] = (f32(x1[j]) + (total + f32(bd_ref[:, cols]))).astype(jnp.bfloat16)
-
-    scatter(down_part, down_finish)
+        x1[j] = (xb[j] + total).astype(jnp.bfloat16)
+        store(j).start()
+
+    scatter(down_part, down_finish, LAGS_DOWN)
     scatter_drain()
+    for j in range(nch):
+        store(j).wait()
 
 
 def solution(mesh):
@@ -290,15 +321,20 @@
         n_tok, side, half = rows * n_dev, rows * n_dev // 2, rows // 2
         bf, fl = jnp.bfloat16, jnp.float32
         row = lambda v: v.reshape(1, -1)
-        vmem = pl.BlockSpec(memory_space=pltpu.VMEM)
         hbm = pl.BlockSpec(memory_space=pl.ANY)
         dma = pltpu.SemaphoreType.DMA
         out = pl.pallas_call(
             functools.partial(layer_kernel, n_dev),
             out_shape=jax.ShapeDtypeStruct((rows, dim), bf),
-            in_specs=[vmem, vmem, vmem, hbm, vmem, hbm, vmem, vmem, vmem, hbm, vmem, hbm, vmem],
-            out_specs=vmem,
+            in_specs=[hbm] * 13,
+            out_specs=hbm,
             scratch_shapes=[
+                pltpu.VMEM((rows, dim), bf),
+                pltpu.VMEM((1, dim), fl), pltpu.VMEM((1, dim), fl),
+                pltpu.VMEM((1, dim), fl), pltpu.VMEM((1, dim), fl),
+                pltpu.VMEM((heads, three, hd), bf), pltpu.VMEM((dim,), bf),
+                pltpu.VMEM((ff,), bf), pltpu.VMEM((dim,), bf),
+                pltpu.VMEM((nch, rows, CH), fl),
                 pltpu.VMEM((nch, n_tok, CH), bf),
                 pltpu.VMEM((nch, CH, ff), bf),
                 pltpu.VMEM((N_WD, ff, CH), bf),
@@ -314,7 +350,7 @@
                 pltpu.VMEM((2, nch, rows, CH), bf),
                 pltpu.VMEM((2, nch, rows, CH), bf),
                 pltpu.VMEM((nch, rows, CH), bf),
-                dma((nch,)), dma(()), dma((N_WD,)),
+                dma((3,)), dma((6,)), dma((nch,)), dma(()), dma((N_WD,)), dma((nch,)),
                 dma(()), dma((nch,)), dma((nch,)), dma((nch,)), dma((nch,)), dma((nch,)),
                 dma(()), dma((nch,)), dma((nch,)), dma((nch,)), dma((nch,)), dma((nch,)),
             ],
@@ -323,8 +359,9 @@
             name="decoder_layer",
         )(
             hidden[0], row(g1), row(s1),
-            jnp.transpose(w_qkv, (1, 2, 0, 3)).reshape(three * heads, dim, hd), row(b_qkv),
-            w_out.reshape(heads * hd, dim), row(b_out), row(g2), row(s2), w_up, row(b_up), w_down, row(b_down),
+            jnp.transpose(w_qkv, (1, 2, 0, 3)).reshape(three * heads, dim, hd),
+            jnp.transpose(b_qkv, (1, 0, 2)),
+            w_out.reshape(heads * hd, dim), b_out, row(g2), row(s2), w_up, b_up, w_down, b_down,
         )
         return out[None]
 

time: 99.7 us -> 80 us (0.80)
  Pallas kernels: 92.3 us -> 78.2 us
  local copies, waits for them, and re-layouts: 6.96 us -> 1.72 us
    pallas_call x1, Pallas kernels: 92.3 us -> 78.2 us  [body(): pl.pallas_call(functools.partial(layer_kernel, n_dev), out_shape=jax.Shap...]
    reshape x4 -> x0, local copies, waits for them, and re-layouts: 4.55 us -> none  [body(): row = lambda v: v.reshape(1, -1)]
    unnamed x2 -> x1, local copies, waits for them, and re-layouts: 2.41 us -> 1.72 us
where the time goes in v2:
time: 80 us; the launch traced here: 79.9 us
  Pallas kernels  78.2 us (98%)
  local copies, waits for them, and re-layouts  1.72 us (2%)
    pallas_call x1, Pallas kernels, body(): pl.pallas_call(functools.partial(layer_kernel, n_dev), out_shape=jax.Shap...  78.2 us
    unnamed x1, local copies, waits for them, and re-layouts  1.72 us

profile of v2, /device:TPU:81, one launch (start us, length us, event | category | flops | bytes accessed | tf_op | source)
XLA Modules:
  0.0 79.9 jit_solution(4299641448022354510)
XLA Ops:
  0.0 78.2 %decoder_layer.1 = bf16[32,5120]{1,0:T(8,128)(2,1)} custom-call(bf16[32,5120]{1,0:T(8,128)(2,1)} %bitcast.14, f32[1,5120]{1,0:T(1,128)} %bitcast.15, f32[1,5120]{1,0:T(1,128)} %bitcast.16, bf16[15,5120,128]{2,1,0:T(8,128)(2,1)} %bitcast.11, bf16[5,3,128]{2,1,0:T(4,128)(2,1)} %bitcast.19, bf16[640,5120]{1,0:T(8,128)(2,1)} %bitcast.12, ...), custom_call_target="tpu_custom_call" | custom-call | tf_op jit(solution)/shard_map/decoder_layer/pallas_call | solution.py:326
  78.2 1.7 %copy.15 = bf16[1,32,5120]{2,1,0:T(8,128)(2,1)} copy(bf16[1,32,5120]{2,1,0:T(8,128)(2,1)} %bitcast.13) | data formatting | bytes 655360

commit v3 on v2

v3 whole, which is shorter than its diff:
```python
import functools

import jax
import jax.numpy as jnp
from jax import lax
from jax.experimental import pallas as pl
from jax.experimental.pallas import tpu as pltpu
from jax.sharding import PartitionSpec as P

LN_EPS = 1e-5
MESH = pl.DeviceIdType.MESH
CH = 512
LOOK = 5
LAG_B, LAG_C = 5, 6
LAGS_OUT = (2, 6, 11)
LAGS_DOWN = (2, 6, 10)
N_WD = 3


def f32(v):
    return v.astype(jnp.float32)


def bf16(v):
    return v.astype(jnp.bfloat16)


def dot(a, b):
    return jnp.dot(a, b, preferred_element_type=jnp.float32)


def layer_kernel(
    n_dev,
    x_hbm, g1_hbm, s1_hbm, wqkv, bqkv_hbm, wo, bo_hbm, g2_hbm, s2_hbm, wu, bu_hbm, wd, bd_hbm,
    out_hbm,
    x_ref, g1_ref, s1_ref, g2_ref, s2_ref, bqkv_ref, bo_ref, bu_ref, bd_ref,
    xb, h_all, u_w, d_w, o_w, acc, qkv, ctx, act, psend, precv,
    hop_s, hop_r, fin_s, fin_r, x1,
    xsem, psem, usem, osem, dsem, outsem, ag_send, ag_l, ag_r, ag_l2, ag_r2, ag_p,
    rs_send, rs_p, rs_hl, rs_hr, rs_fl, rs_fr,
):
    small = [pltpu.make_async_copy(a, b, xsem.at[i]) for i, (a, b) in enumerate(
        ((x_hbm, x_ref), (g1_hbm, g1_ref), (s1_hbm, s1_ref)))]
    late = [pltpu.make_async_copy(a, b, psem.at[i]) for i, (a, b) in enumerate(
        ((bqkv_hbm, bqkv_ref), (bo_hbm, bo_ref), (g2_hbm, g2_ref), (s2_hbm, s2_ref), (bu_hbm, bu_ref), (bd_hbm, bd_ref)))]
    for copy in small:
        copy.start()
    n_chips = n_dev // 2
    rows, dim = x_ref.shape
    nch = dim // CH
    ng = nch // 2
    hr = rows // 2
    side = hr * n_chips
    st_rows = 2 * side
    n_tok = 2 * st_rows
    hc = CH // 2
    n_slab = wqkv.shape[0]
    hd = wqkv.shape[2]
    heads = n_slab // 3
    qw = n_slab * hd
    ff = wu.shape[1]
    nt = ff // CH
    me = lax.axis_index("tp")
    chip, core = me // 2, me % 2
    right = {"tp": ((chip + 1) % n_chips) * 2 + core}
    left = {"tp": ((chip + n_chips - 1) % n_chips) * 2 + core}
    mate = {"tp": chip * 2 + (1 - core)}

    def push(src, dst, ssem, rsem, dev):
        return pltpu.make_async_remote_copy(
            src_ref=src, dst_ref=dst, send_sem=ssem, recv_sem=rsem, device_id=dev, device_id_type=MESH)

    barrier = pltpu.get_barrier_semaphore()
    for dev in (left, right, mate):
        pl.semaphore_signal(barrier, inc=1, device_id=dev, device_id_type=MESH)

    def load_qkv(j):
        for s in range(n_slab):
            pltpu.make_async_copy(
                wqkv.at[s, pl.ds(pl.multiple_of(j * CH, CH), CH), :],
                u_w.at[j, :, pl.ds(s * hd, hd)], usem.at[j]).start()

    def load_up(j):
        return pltpu.make_async_copy(
            wu.at[pl.ds(pl.multiple_of(j * CH, CH), CH), :], u_w.at[j], usem.at[j])

    def load_down(q):
        g, slot = q % ng, q % N_WD
        return pltpu.make_async_copy(
            wd.at[:, pl.ds(pl.multiple_of(g * 2 * CH, 2 * CH), 2 * CH)], d_w.at[slot], dsem.at[slot])

    def init_loads(j, c):
        load_qkv(j)
        return c

    lax.fori_loop(0, nch, init_loads, 0)
    for copy in late:
        copy.start()
    out_load = pltpu.make_async_copy(wo, o_w, osem)
    out_load.start()
    for q in range(N_WD):
        load_down(q).start()

    def norm(get, put, n, gain_ref, shift_ref):
        tot = jnp.zeros((n, CH), jnp.float32)
        for j in range(nch):
            tot += get(j)
        mean = jnp.sum(tot, axis=1, keepdims=True) * (1.0 / dim)
        tot = jnp.zeros((n, CH), jnp.float32)
        for j in range(nch):
            cen = get(j) - mean
            tot += cen * cen
        var = jnp.sum(tot, axis=1, keepdims=True) * (1.0 / dim)
        inv = lax.rsqrt(var + LN_EPS)
        for j in range(nch):
            cols = slice(j * CH, (j + 1) * CH)
            put(j, bf16((get(j) - mean) * inv * gain_ref[:, cols] + shift_ref[:, cols]))

    def put_both(j, y):
        h_all[j, 0, 0:hr, :] = y[0:hr]
        h_all[j, 1, 0:hr, :] = y[hr:]

    def put_stream(st):
        def put(j, y):
            h_all[j, st, 0:hr, :] = y
        return put

    for copy in small:
        copy.wait()
    norm(lambda j: f32(x_ref[:, j * CH:(j + 1) * CH]), put_both, rows, g1_ref, s1_ref)
    acc[...] = jnp.zeros_like(acc)
    pl.semaphore_wait(barrier, 3)

    def piece_both(v, s, r, lo=0, n=CH):
        return h_all.at[v, :, pl.ds(s * side + r * hr, hr), pl.ds(lo, n)]

    def all_both(v, s):
        return h_all.at[v, :, pl.ds(s * side, side), :]

    def piece_stream(v, s, r, lo=0, n=CH):
        return h_all.at[pl.ds((v % ng) * 2, 2), v // ng, pl.ds(s * side + r * hr, hr), pl.ds(lo, n)]

    def all_stream(v, s):
        return h_all.at[pl.ds((v % ng) * 2, 2), v // ng, pl.ds(s * side, side), :]

    def send_own(at, v):
        push(at(v, 0, 0), at(v, 0, 3), ag_send, ag_l.at[v], right).start()
        push(at(v, 0, 0), at(v, 0, 1), ag_send, ag_r.at[v], left).start()
        push(at(v, 0, 0), at(v, 1, 0), ag_send, ag_p.at[v], mate).start()

    def wait_mate(whole, v):
        push(whole(v, 0), whole(v, 1), ag_send, ag_p.at[v], mate).wait_recv()

    def gather(at, whole, n_use, consume, steps):
        def step(i, c):
            @pl.when(i + LOOK < nch)
            def _():
                send_own(at, i + LOOK)

            @pl.when(i < nch)
            def _():
                with jax.named_scope("gw1l"):
                    push(at(i, 0, 0), at(i, 0, 3), ag_send, ag_l.at[i], right).wait_recv()
                push(at(i, 0, 3, 0, hc), at(i, 0, 2, 0, hc), ag_send, ag_l2.at[i], right).start()
                push(at(i, 0, 3), at(i, 1, 3), ag_send, ag_p.at[i], mate).start()
                with jax.named_scope("gw1r"):
                    push(at(i, 0, 0), at(i, 0, 1), ag_send, ag_r.at[i], left).wait_recv()
                push(at(i, 0, 1, hc, hc), at(i, 0, 2, hc, hc), ag_send, ag_r2.at[i], left).start()
                push(at(i, 0, 1), at(i, 1, 1), ag_send, ag_p.at[i], mate).start()

            @pl.when((i >= LAG_B) & (i < nch + LAG_B))
            def _():
                j = i - LAG_B
                with jax.named_scope("gw2"):
                    push(at(j, 0, 3, 0, hc), at(j, 0, 2, 0, hc), ag_send, ag_l2.at[j], right).wait_recv()
                    push(at(j, 0, 1, hc, hc), at(j, 0, 2, hc, hc), ag_send, ag_r2.at[j], left).wait_recv()
                push(at(j, 0, 2), at(j, 1, 2), ag_send, ag_p.at[j], mate).start()

            @pl.when((i >= LAG_C) & (i < n_use + LAG_C))
            def _():
                j = i - LAG_C
                with jax.named_scope("gwp"):
                    wait_mate(whole, j)
                with jax.named_scope("guse"):
                    consume(j)
            return c

        lax.fori_loop(0, steps, step, 0)

    def gather_drain():
        sent = h_all.at[:, :, pl.ds(0, 7 * hr), :]
        push(sent, sent, ag_send, ag_p.at[0], mate).wait_send()

    tiles = [(t, min(CH, qw - t * CH)) for t in range((qw + CH - 1) // CH)]

    def use_qkv(j):
        pltpu.make_async_copy(u_w.at[j, :, pl.ds(0, qw)], u_w.at[j, :, pl.ds(0, qw)], usem.at[j]).wait()
        h = h_all[j].reshape(n_tok, CH)
        for t, n in tiles:
            p = dot(h, u_w[j, :, t * CH:t * CH + n])
            acc[2 * t, :, 0:n] += p[0:st_rows]
            acc[2 * t + 1, :, 0:n] += p[st_rows:]
        load_up(j).start()

    for v in range(LOOK):
        send_own(piece_both, v)
    with jax.named_scope("gather1"):
        gather(piece_both, all_both, nch, use_qkv, nch + LAG_C)
    for copy in late:
        copy.wait()
    for s in range(n_slab):
        lo = s * hd
        for st in range(2):
            part = acc[2 * (lo // CH) + st, :, lo % CH:lo % CH + hd]
            qkv[st * st_rows:(st + 1) * st_rows, lo:lo + hd] = bf16(
                part + f32(bqkv_ref[s % heads, s // heads:s // heads + 1, :]))

    def position(i):
        st, s, r, w = i // st_rows, (i // side) % 2, (i // hr) % n_chips, i % hr
        return ((chip + r) % n_chips) * (2 * rows) + (core + s - 2 * core * s) * rows + st * hr + w

    qpos = position(lax.broadcasted_iota(jnp.int32, (n_tok, n_tok), 0))
    kpos = position(lax.broadcasted_iota(jnp.int32, (n_tok, n_tok), 1))
    keep = qpos >= kpos
    for h in range(heads):
        q = qkv[:, h * hd:(h + 1) * hd]
        k = qkv[:, (heads + h) * hd:(heads + h + 1) * hd]
        v = qkv[:, (2 * heads + h) * hd:(2 * heads + h + 1) * hd]
        logits = lax.dot_general(q, k, (((1,), (1,)), ((), ())), preferred_element_type=jnp.float32) * hd ** -0.5
        logits = jnp.where(keep, logits, -1e30)
        e = jnp.exp(logits - jnp.max(logits, axis=1, keepdims=True))
        p = bf16(e / jnp.sum(e, axis=1, keepdims=True))
        ctx[:, h * hd:(h + 1) * hd] = bf16(dot(p, v))

    gather_drain()
    out_load.wait()

    def pair_sum(v, st, g):
        for c in range(2):
            j = 2 * g + c
            s = acc[v, c * side:(c + 1) * side, :] + f32(precv[st, j])
            two = bf16(s[2 * hr:3 * hr])
            hop_s[0, st, j] = two[:, 0:hc]
            hop_s[1, st, j] = two[:, hc:]
            acc[v, c * side:(c + 1) * side, :] = s

    def middle_sum(v, st, g):
        for c in range(2):
            j = 2 * g + c
            one = acc[v, c * side + hr:c * side + 2 * hr, :]
            fin_s[0, st, j, :, 0:hc] = bf16(one[:, 0:hc] + f32(hop_r[0, st, j]))
            fin_s[0, st, j, :, hc:] = bf16(one[:, hc:])
            three = acc[v, c * side + 3 * hr:(c + 1) * side, :]
            fin_s[1, st, j, :, 0:hc] = bf16(three[:, 0:hc])
            fin_s[1, st, j, :, hc:] = bf16(three[:, hc:] + f32(hop_r[1, st, j]))

    def fins(st, g, v):
        pair = pl.ds(2 * g, 2)
        return (push(fin_s.at[0, st, pair], fin_r.at[0, st, pair], rs_send, rs_fl.at[v], right),
                push(fin_s.at[1, st, pair], fin_r.at[1, st, pair], rs_send, rs_fr.at[v], left))

    def last_sum(v, st, g):
        for copy in fins(st, g, v):
            copy.wait_recv()
        for c in range(2):
            j = 2 * g + c
            total = acc[v, c * side:c * side + hr, :] + f32(fin_r[0, st, j]) + f32(fin_r[1, st, j])
            x1[st, j] = bf16(xb[st, j] + total)

    def scatter_drain():
        push(psend, precv, rs_send, rs_p.at[0], mate).wait_send()
        push(hop_s, hop_r, rs_send, rs_p.at[0], mate).wait_send()
        push(fin_s, fin_r, rs_send, rs_p.at[0], mate).wait_send()

    bo = f32(bo_ref[...]).reshape(1, dim)
    for j in range(nch):
        cols = slice(j * CH, (j + 1) * CH)
        y = f32(x_ref[:, cols]) + bo[:, cols]
        xb[0, j] = y[0:hr]
        xb[1, j] = y[hr:]

    def pairs_out(g):
        two = pl.ds(2 * g, 2)
        return push(psend.at[:, two], precv.at[:, two], rs_send, rs_p.at[g], mate)

    def hops_out(g):
        two = pl.ds(2 * g, 2)
        return (push(hop_s.at[0, :, two], hop_r.at[0, :, two], rs_send, rs_hl.at[g], right),
                push(hop_s.at[1, :, two], hop_r.at[1, :, two], rs_send, rs_hr.at[g], left))

    lag_p, lag_h, lag_f = LAGS_OUT

    def out_step(i, carry):
        @pl.when(i < ng)
        def _():
            with jax.named_scope("spart"):
                for c in range(2):
                    j = 2 * i + c
                    p = dot(ctx[...], o_w[:, pl.ds(pl.multiple_of(j * CH, CH), CH)])
                    for st in range(2):
                        acc[st * ng + i, c * side:(c + 1) * side, :] = p[st * st_rows:st * st_rows + side]
                        psend[st, j] = bf16(p[st * st_rows + side:(st + 1) * st_rows])
            pairs_out(i).start()

        @pl.when((i >= lag_p) & (i < ng + lag_p))
        def _():
            g = i - lag_p
            with jax.named_scope("swp"):
                pairs_out(g).wait_recv()
            for st in range(2):
                pair_sum(st * ng + g, st, g)
            for copy in hops_out(g):
                copy.start()

        @pl.when((i >= lag_h) & (i < ng + lag_h))
        def _():
            g = i - lag_h
            with jax.named_scope("swh"):
                for copy in hops_out(g):
                    copy.wait_recv()
            for st in range(2):
                middle_sum(st * ng + g, st, g)
            for copy in fins(0, g, g):
                copy.start()

        @pl.when(i == ng + lag_h - 1)
        def _():
            for g in range(ng):
                for copy in fins(1, g, ng + g):
                    copy.start()

        @pl.when(i >= lag_f)
        def _():
            g = i - lag_f
            with jax.named_scope("swf"):
                last_sum(g, 0, g)
        return carry

    with jax.named_scope("scatter1"):
        lax.fori_loop(0, ng + lag_f, out_step, 0)

    with jax.named_scope("ln2a"):
        norm(lambda j: f32(x1[0, j]), put_stream(0), hr, g2_ref, s2_ref)
    for v in range(LOOK):
        send_own(piece_stream, v)

    def last_out(g, carry):
        last_sum(ng + g, 1, g)
        return carry

    with jax.named_scope("last1"):
        lax.fori_loop(0, ng, last_out, 0)
    with jax.named_scope("ln2b"):
        norm(lambda j: f32(x1[1, j]), put_stream(1), hr, g2_ref, s2_ref)
    acc[ng:2 * ng] = jnp.zeros((ng, st_rows, CH), jnp.float32)
    bd = f32(bd_ref[...]).reshape(1, dim)
    for j in range(nch):
        for st in range(2):
            xb[st, j] = f32(x1[st, j]) + bd[:, j * CH:(j + 1) * CH]
    for j in range(nch):
        load_up(j).wait()

    def use_up(v):
        st, g = v // ng, v % ng
        h = jnp.concatenate([h_all[2 * g, st], h_all[2 * g + 1, st]], axis=1)
        for t in range(nt):
            w = u_w[pl.ds(2 * g, 2), :, t * CH:(t + 1) * CH].reshape(2 * CH, CH)
            acc[ng + t] += dot(h, w)

    with jax.named_scope("gather2"):
        gather(piece_stream, all_stream, ng, use_up, nch + LAG_B)
    scatter_drain()

    bu = f32(bu_ref[...]).reshape(1, ff)

    def activate(st):
        for t in range(nt):
            cols = slice(t * CH, (t + 1) * CH)
            act[st, :, cols] = bf16(jax.nn.gelu(acc[ng + t] + bu[:, cols], approximate=True))
            acc[ng + t] = jnp.zeros((st_rows, CH), jnp.float32)

    def store(st, j):
        return pltpu.make_async_copy(
            x1.at[st, j],
            out_hbm.at[pl.ds(pl.multiple_of(st * hr, hr), hr), pl.ds(pl.multiple_of(j * CH, CH), CH)], outsem)

    def pairs_down(v, st, g):
        two = pl.ds(2 * g, 2)
        return push(psend.at[st, two], precv.at[st, two], rs_send, rs_p.at[v], mate)

    def hops_down(v, st, g):
        two = pl.ds(2 * g, 2)
        return (push(hop_s.at[0, st, two], hop_r.at[0, st, two], rs_send, rs_hl.at[v], right),
                push(hop_s.at[1, st, two], hop_r.at[1, st, two], rs_send, rs_hr.at[v], left))

    def when_group(k, fn):
        @pl.when(((k >= 0) & (k < ng)) | ((k >= 2 * ng) & (k < 3 * ng)))
        def _():
            st = k // (2 * ng)
            g = k - st * 2 * ng
            fn(st * ng + g, st, g)

    lag_p2, lag_h2, lag_f2 = LAGS_DOWN

    def down_part(v, st, g):
        load_down(v).wait()
        slot = v % N_WD
        with jax.named_scope("dpart"):
            for c in range(2):
                j = 2 * g + c
                p = dot(act[st], d_w[slot, :, c * CH:(c + 1) * CH])
                acc[v, c * side:(c + 1) * side, :] = p[0:side]
                psend[st, j] = bf16(p[side:])

        @pl.when(v + N_WD < 2 * ng)
        def _():
            load_down(v + N_WD).start()
        pairs_down(v, st, g).start()

    def down_pair(v, st, g):
        with jax.named_scope("dwp"):
            pairs_down(v, st, g).wait_recv()
        pair_sum(v, st, g)
        for copy in hops_down(v, st, g):
            copy.start()

    def down_middle(v, st, g):
        with jax.named_scope("dwh"):
            for copy in hops_down(v, st, g):
                copy.wait_recv()
        middle_sum(v, st, g)
        for copy in fins(st, g, v):
            copy.start()

    def down_last(v, st, g):
        with jax.named_scope("dwf"):
            last_sum(v, st, g)
        for c in range(2):
            store(st, 2 * g + c).start()

    def mlp_step(w, carry):
        @pl.when((w == 0) | (w == 2 * ng))
        def _():
            with jax.named_scope("gelu"):
                activate(w // (2 * ng))

        when_group(w, down_part)

        @pl.when((w >= ng) & (w < 2 * ng))
        def _():
            with jax.named_scope("mwp"):
                wait_mate(all_stream, w)
            with jax.named_scope("muse"):
                use_up(w)

        when_group(w - lag_p2, down_pair)
        when_group(w - lag_h2, down_middle)
        when_group(w - lag_f2, down_last)
        return carry

    with jax.named_scope("mlp"):
        lax.fori_loop(0, 3 * ng + lag_f2, mlp_step, 0)
    scatter_drain()
    gather_drain()
    pltpu.make_async_copy(x1, x1, outsem).wait()


def solution(mesh):
    n_dev = mesh.shape["tp"]

    def body(hidden, g1, s1, w_qkv, b_qkv, w_out, b_out, g2, s2, w_up, b_up, w_down, b_down):
        _, rows, dim = hidden.shape
        _, three, heads, hd = w_qkv.shape
        ff = w_up.shape[1]
        nch = dim // CH
        n_tok, hr = rows * n_dev, rows // 2
        st_rows, side = n_tok // 2, n_tok // 4
        bf, fl = jnp.bfloat16, jnp.float32
        row = lambda v: v.reshape(1, -1)
        hbm = pl.BlockSpec(memory_space=pl.ANY)
        dma = pltpu.SemaphoreType.DMA
        out = pl.pallas_call(
            functools.partial(layer_kernel, n_dev),
            out_shape=jax.ShapeDtypeStruct((rows, dim), bf),
            in_specs=[hbm] * 13,
            out_specs=hbm,
            scratch_shapes=[
                pltpu.VMEM((rows, dim), bf),
                pltpu.VMEM((1, dim), fl), pltpu.VMEM((1, dim), fl),
                pltpu.VMEM((1, dim), fl), pltpu.VMEM((1, dim), fl),
                pltpu.VMEM((heads, three, hd), bf), pltpu.VMEM((dim,), bf),
                pltpu.VMEM((ff,), bf), pltpu.VMEM((dim,), bf),
                pltpu.VMEM((2, nch, hr, CH), fl),
                pltpu.VMEM((nch, 2, st_rows, CH), bf),
                pltpu.VMEM((nch, CH, ff), bf),
                pltpu.VMEM((N_WD, ff, 2 * CH), bf),
                pltpu.VMEM((heads * hd, dim), bf),
                pltpu.VMEM((nch, st_rows, CH), fl),
                pltpu.VMEM((n_tok, three * heads * hd), bf),
                pltpu.VMEM((n_tok, heads * hd), bf),
                pltpu.VMEM((2, st_rows, ff), bf),
                pltpu.VMEM((2, nch, side, CH), bf),
                pltpu.VMEM((2, nch, side, CH), bf),
                pltpu.VMEM((2, 2, nch, hr, CH // 2), bf),
                pltpu.VMEM((2, 2, nch, hr, CH // 2), bf),
                pltpu.VMEM((2, 2, nch, hr, CH), bf),
                pltpu.VMEM((2, 2, nch, hr, CH), bf),
                pltpu.VMEM((2, nch, hr, CH), bf),
                dma((3,)), dma((6,)), dma((nch,)), dma(()), dma((N_WD,)), dma(()),
                dma(()), dma((nch,)), dma((nch,)), dma((nch,)), dma((nch,)), dma((nch,)),
                dma(()), dma((nch,)), dma((nch,)), dma((nch,)), dma((nch,)), dma((nch,)),
            ],
            compiler_params=pltpu.CompilerParams(
                collective_id=0, has_side_effects=True, vmem_limit_bytes=67043328),
            name="decoder_layer",
        )(
            hidden[0], row(g1), row(s1),
            jnp.transpose(w_qkv, (1, 2, 0, 3)).reshape(three * heads, dim, hd),
            jnp.transpose(b_qkv, (1, 0, 2)),
            w_out.reshape(heads * hd, dim), b_out, row(g2), row(s2), w_up, b_up, w_down, b_down,
        )
        return out[None]

    specs = (P("dp", "tp", None), P(), P(), P(None, None, "tp", None), P(None, "tp", None),
             P("tp", None, None), P(), P(), P(), P(None, "tp"), P("tp"), P("tp", None), P())
    return jax.shard_map(body, mesh=mesh, in_specs=specs, out_specs=P("dp", "tp", None), check_vma=False)
```

time: 80 us -> 80.2 us (level)
  no operation moved by 1% of the time
where the time goes in v3:
time: 80.2 us; the launch traced here: 80 us
  Pallas kernels  78.3 us (98%)
  local copies, waits for them, and re-layouts  1.72 us (2%)
    pallas_call x1, Pallas kernels, body(): pl.pallas_call(functools.partial(layer_kernel, n_dev), out_shape=jax.Shap...  78.3 us
    unnamed x1, local copies, waits for them, and re-layouts  1.72 us

profile of v3, /device:TPU:81, one launch (start us, length us, event | category | flops | bytes accessed | tf_op | source)
XLA Modules:
  0.0 80.0 jit_solution(7553143532632185150)
XLA Ops:
  0.0 78.3 %decoder_layer.1 = bf16[32,5120]{1,0:T(8,128)(2,1)} custom-call(bf16[32,5120]{1,0:T(8,128)(2,1)} %bitcast.14, f32[1,5120]{1,0:T(1,128)} %bitcast.15, f32[1,5120]{1,0:T(1,128)} %bitcast.16, bf16[15,5120,128]{2,1,0:T(8,128)(2,1)} %bitcast.11, bf16[5,3,128]{2,1,0:T(4,128)(2,1)} %bitcast.19, bf16[640,5120]{1,0:T(8,128)(2,1)} %bitcast.12, ...), custom_call_target="tpu_custom_call" | custom-call | tf_op jit(solution)/shard_map/decoder_layer/pallas_call | solution.py:482
  78.3 1.7 %copy.15 = bf16[1,32,5120]{2,1,0:T(8,128)(2,1)} copy(bf16[1,32,5120]{2,1,0:T(8,128)(2,1)} %bitcast.13) | data formatting | bytes 655360
